TPU v7x, 32 devices: a whole 2x2x4 slice. The times are simulated.
32 devices in a mesh: tok: 8 (over y, x, core), slot: 4 (over z).
Axes of the slice: x: 2, y: 2, z: 4, core: 2. Of those that a mesh axis runs over, the one named last changes fastest.
Arguments:
- tokens: bfloat16 [8192, 1024], P('tok'), may hold values from -16 to 16
- slot_params: bfloat16 [8192, 1024], P('slot'), may hold values from -0.5 to 0.5
- w_in: bfloat16 [16, 1024, 4096], P('slot', None, 'tok'), may hold values from -0.1875 to 0.1875
- w_out: bfloat16 [16, 4096, 1024], P('slot', 'tok'), may hold values from -0.09375 to 0.09375
Outputs:
- mixed: bfloat16 [8192, 1024], P(('tok', 'slot'))
All inputs are finite; a program needn't handle non-finite values.
Results may differ from a plain program's by a relative error of at most 0.01.
Values may be sent and summed in bfloat16 or wider, within the bound.
No kernel may reach another device: no remote copies, remote signals or barrier semaphores. Data moves between devices by JAX's collectives and lax.ppermute only.
A program may use at most 64 MiB of HBM per device.

v0:
```python
import jax
import jax.numpy as jnp
from jax import lax
from jax.sharding import PartitionSpec as P

P_SIZE = 8


def body(tokens, slot_params, w_in, w_out):
    experts_here = w_in.shape[0]
    in_flight = experts_here * P_SIZE
    logits = lax.dot_general(
        slot_params, tokens, (((1,), (1,)), ((), ())), preferred_element_type=jnp.float32
    )
    flight = logits[:in_flight]
    col_max = lax.pmax(jnp.max(flight, axis=1), "tok")
    dispatch_exp = jnp.exp(flight - col_max[:, None])
    dispatch_w = dispatch_exp.astype(jnp.bfloat16)
    numer = jnp.dot(dispatch_w, tokens, preferred_element_type=jnp.float32)
    numer, totals = lax.psum((numer, jnp.sum(dispatch_exp, axis=1)), "tok")
    slot_in = (
        (numer / totals[:, None]).astype(jnp.bfloat16).reshape(experts_here, P_SIZE, numer.shape[1])
    )
    pre_act = jnp.einsum("epd,edh->eph", slot_in, w_in, preferred_element_type=jnp.float32)
    hidden = jax.nn.gelu(pre_act).astype(jnp.bfloat16)
    partial_out = jnp.einsum("eph,ehd->epd", hidden, w_out, preferred_element_type=jnp.float32)
    partial_out = partial_out.reshape(in_flight, partial_out.shape[2])
    slot_out = lax.psum(partial_out, "tok").astype(jnp.bfloat16)
    row_max = lax.pmax(jnp.max(logits, axis=0), "slot")
    row_sum = lax.psum(jnp.sum(jnp.exp(logits - row_max[None, :]), axis=0), "slot")
    combine_w = (jnp.exp(flight - row_max[None, :]) / row_sum[None, :]).astype(jnp.bfloat16)
    token_weights = lax.all_to_all(combine_w, "slot", split_axis=1, concat_axis=0, tiled=True)
    all_outputs = lax.all_gather(slot_out, "slot", axis=0, tiled=True)
    mixed = lax.dot_general(
        token_weights, all_outputs, (((0,), (0,)), ((), ())), preferred_element_type=jnp.float32
    )
    return mixed.astype(jnp.bfloat16)


def solution(mesh):
    return jax.shard_map(
        body,
        mesh=mesh,
        in_specs=(P("tok", None), P("slot", None), P("slot", None, "tok"), P("slot", "tok", None)),
        out_specs=P(("tok", "slot"), None),
        check_vma=False,
    )
```

profile of v0, /device:TPU:0, one launch (start us, length us, event | category | flops | bytes accessed | tf_op | source)
XLA Modules:
  0.0 138.5 jit_solution(10838787701703055438)
XLA Ops:
  6.5 0.0 copy-start
  6.5 0.0 all-reduce.3.cloned.1.call-start
  6.5 1.6 %copy-done = bf16[1024,1024]{1,0:T(8,128)(2,1)S(1)} copy-done((bf16[1024,1024]{1,0:T(8,128)(2,1)S(1)}, bf16[1024,1024]{1,0:T(8,128)(2,1)}, u32[]{:S(2)}) %copy-start) | copy-done | bytes 2097176
  8.1 6.4 %fusion.27 = (f32[1024]{0:T(1024)S(1)}, f32[2048,1024]{1,0:T(8,128)S(1)}) fusion(bf16[2048,1024]{1,0:T(8,128)(2,1)} %param.5, bf16[1024,1024]{1,0:T(8,128)(2,1)S(1)} %copy-done), kind=kOutput, calls=%fused_computation.31 | convolution fusion | flops 4297063424 | bytes 14684160 | tf_op jit(solution)/shard_map/dot_general | solution.py:12
  14.5 0.0 copy-start.1
  14.5 3.2 %copy-done.1 = f32[2048,1024]{1,0:T(8,128)} copy-done((f32[2048,1024]{1,0:T(8,128)}, f32[2048,1024]{1,0:T(8,128)S(1)}, u32[]{:S(2)}) %copy-start.1) | copy-done | bytes 8388632
  17.7 0.1 slice_reduce_fusion
  17.8 15.2 %pmax.15 = f32[32]{0:T(128)S(1)} all-reduce(f32[32]{0:T(128)S(1)} %slice_reduce_fusion), channel_id=1, replica_groups=mesh['tok'=8,'slot'=4] {'tok'}, use_global_device_ids=true, to_apply=%region_5.0 | all-reduce | flops 32 | bytes 256 | tf_op jit(solution)/shard_map/pmax | solution.py:16
  33.0 2.1 %fusion.10 = f32[32,1024]{1,0:T(8,128)} fusion(bf16[1024,1024]{1,0:T(8,128)(2,1)S(1)} %copy-done, f32[2048,1024]{1,0:T(8,128)} %copy-done.1, f32[32]{0:T(128)S(1)} %pmax.15), kind=kOutput, calls=%fused_computation.18 | convolution fusion | flops 67174400 | bytes 2359424 | tf_op jit(solution)/shard_map/dot_general | solution.py:19
  35.1 0.0 all-reduce.3.cloned.1.call-update
  35.1 12.0 %pmax.14 = f32[1024]{0:T(1024)S(1)} all-reduce(f32[1024]{0:T(1024)S(1)} %get-tuple-element.7), channel_id=1, replica_groups=mesh['tok'=8,'slot'=4] {'slot'}, use_global_device_ids=true, to_apply=%region_1.0 | all-reduce | flops 1024 | bytes 8192 | tf_op jit(solution)/shard_map/pmax | solution.py:29
  47.1 4.6 %exponential_reduce_fusion = f32[1024]{0:T(1024)S(1)} fusion(f32[2048,1024]{1,0:T(8,128)} %copy-done.1, f32[1024]{0:T(1024)S(1)} %pmax.14), kind=kLoop, calls=%fused_computation | loop fusion | flops 4193280 | bytes 8396800 | tf_op jit(solution)/shard_map/reduce_sum | solution.py:30
  51.6 8.4 %psum.28 = f32[1024]{0:T(1024)S(1)} all-reduce(f32[1024]{0:T(1024)S(1)} %exponential_reduce_fusion), channel_id=1, replica_groups=mesh['tok'=8,'slot'=4] {'slot'}, use_global_device_ids=true, to_apply=%region_3.0 | all-reduce | flops 1024 | bytes 8192 | tf_op jit(solution)/shard_map/psum | solution.py:30
  60.0 1.1 fusion
  61.1 0.6 copy.8
  61.8 3.3 %all-to-all-start = ((bf16[32,4,256]{2,0,1:T(8,128)(2,1)}), bf16[32,4,256]{2,0,1:T(8,128)(2,1)S(1)}, u32[]{:S(2)}, u32[]{:S(2)}) async-start(bf16[32,4,256]{2,0,1:T(8,128)(2,1)} %bitcast.22), calls=%async_computation | async-start | bytes 131072 | tf_op jit(solution)/shard_map/all_to_all | solution.py:32
  65.0 11.9 %psum.30 = f32[32]{0:T(128)S(1)} all-reduce(f32[32]{0:T(128)S(1)} %get-tuple-element.5), channel_id=1, replica_groups=mesh['tok'=8,'slot'=4] {'tok'}, use_global_device_ids=true, to_apply=%region_8.0 | all-reduce | flops 32 | bytes 256 | tf_op jit(solution)/shard_map/psum | solution.py:20
  76.9 11.1 %all-reduce.3.cloned.1.call-done = f32[32,1024]{1,0:T(8,128)} async-done(((f32[32,1024]{1,0:T(8,128)}), f32[32,1024]{1,0:T(8,128)}) %all-reduce.3.cloned.1.call-update) | async-done | bytes 131088 | tf_op jit(solution)/shard_map/psum | solution.py:20
  88.1 4.7 %convolution_bitcast_fusion = f32[32,1024]{1,0:T(8,128)S(1)} fusion(bf16[4,512,1024]{2,1,0:T(8,128)(2,1)} %param.7, bf16[4,1024,512]{2,1,0:T(8,128)(2,1)} %param.6, f32[32,1024]{1,0:T(8,128)} %all-reduce.3.cloned.1.call-done, f32[32]{0:T(128)S(1)} %psum.30), kind=kOutput, calls=%fused_computation.2 | convolution fusion | flops 67321856 | bytes 8650880 | tf_op jit(solution)/shard_map/eph,ehd->epd/dot_general | solution.py:26
  92.8 23.4 %all-reduce.4 = bf16[32,1024]{1,0:T(8,128)(2,1)S(1)} all-reduce(f32[32,1024]{1,0:T(8,128)S(1)} %convolution_bitcast_fusion), channel_id=1, replica_groups=mesh['tok'=8,'slot'=4] {'tok'}, use_global_device_ids=true, to_apply=%region_9.0 | all-reduce | flops 32768 | bytes 196608 | tf_op jit(solution)/shard_map/psum | solution.py:28
  116.3 14.3 %all_gather.3 = bf16[128,1024]{1,0:T(8,128)(2,1)S(1)} all-gather(bf16[32,1024]{1,0:T(8,128)(2,1)S(1)} %all-reduce.4), channel_id=1, replica_groups=mesh['tok'=8,'slot'=4] {'slot'}, dimensions={0}, use_global_device_ids=true | all-gather | bytes 327680 | tf_op jit(solution)/shard_map/all_gather | solution.py:33
  130.6 0.0 all-to-all-done
  130.6 1.1 convolution_convert_fusion
Async XLA Ops:
  6.5 1.6 %copy-start = (bf16[1024,1024]{1,0:T(8,128)(2,1)S(1)}, bf16[1024,1024]{1,0:T(8,128)(2,1)}, u32[]{:S(2)}) copy-start(bf16[1024,1024]{1,0:T(8,128)(2,1)} %param.4) | copy-start | bytes 6291460
  6.5 81.5 %all-reduce.3.cloned.1.call-start = ((), (), s32[]{:S(2)}) async-start(), calls=%async_computation.1 | async-start | bytes 262144 | tf_op jit(solution)/shard_map/psum | solution.py:20
  14.5 3.2 %copy-start.1 = (f32[2048,1024]{1,0:T(8,128)}, f32[2048,1024]{1,0:T(8,128)S(1)}, u32[]{:S(2)}) copy-start(f32[2048,1024]{1,0:T(8,128)S(1)} %get-tuple-element.8) | copy-start | bytes 25165828
  61.8 68.8 %all-to-all-start = ((bf16[32,4,256]{2,0,1:T(8,128)(2,1)}), bf16[32,4,256]{2,0,1:T(8,128)(2,1)S(1)}, u32[]{:S(2)}, u32[]{:S(2)}) async-start(bf16[32,4,256]{2,0,1:T(8,128)(2,1)} %bitcast.22), calls=%async_computation | async-start | bytes 131072 | tf_op jit(solution)/shard_map/all_to_all | solution.py:32
Sparse Core Ops, SparseCore 0:
  35.2 52.7 all-reduce.2
where the time goes:
time: 139 us
  blocking collectives  85.1 us (61%)
  matrix products  14.3 us (10%)
  between operations  13.4 us (10%)
  waiting for transfers between devices  11.1 us (8%)
  other arithmetic  5.79 us (4%)
  local copies, waits for them, and re-layouts  5.43 us (4%)
  starting transfers between devices  3.29 us (2%)
    psum x1, blocking collectives, body(): slot_out = lax.psum(partial_out, 'tok').astype(jnp.bfloat16)  23.4 us
    pmax x1, blocking collectives, body(): col_max = lax.pmax(jnp.max(flight, axis=1), 'tok')  15.2 us
    all_gather x1, blocking collectives, body(): all_outputs = lax.all_gather(slot_out, 'slot', axis=0, tiled=True)  14.3 us
    pmax x1, blocking collectives, body(): row_max = lax.pmax(jnp.max(logits, axis=0), 'slot')  12 us
    psum x1, blocking collectives, body(): numer, totals = lax.psum((numer, jnp.sum(dispatch_exp, axis=1)), 'tok')  11.9 us
    psum x1, waiting for transfers between devices, body(): numer, totals = lax.psum((numer, jnp.sum(dispatch_exp, axis=1)), 'tok')  11.1 us
    psum x1, blocking collectives, body(): lax.psum(jnp.sum(jnp.exp(logits - row_max[None, :]), axis=0), 'slot')  8.37 us
    dot_general x1, matrix products, body(): lax.dot_general(slot_params, tokens, (((1,), (1,)), ((), ())), preferred_...  6.38 us
  transfers between devices with their start and end apart: 2, of which 1 were waited for; matrix products, arithmetic and copies ran while one was open for 8% of the time, Pallas kernels for 0%

commit v1 on v0

--- a/solution.py
+++ b/solution.py
@@ -27,7 +27,9 @@
     partial_out = partial_out.reshape(in_flight, partial_out.shape[2])
     slot_out = lax.psum(partial_out, "tok").astype(jnp.bfloat16)
     row_max = lax.pmax(jnp.max(logits, axis=0), "slot")
-    row_sum = lax.psum(jnp.sum(jnp.exp(logits - row_max[None, :]), axis=0), "slot")
+    own = jnp.sum(jnp.exp(logits - row_max[None, :]), axis=0)
+    pieces = lax.all_gather(own, "slot")
+    row_sum = jnp.sum(pieces, axis=0)
     combine_w = (jnp.exp(flight - row_max[None, :]) / row_sum[None, :]).astype(jnp.bfloat16)
     token_weights = lax.all_to_all(combine_w, "slot", split_axis=1, concat_axis=0, tiled=True)
     all_outputs = lax.all_gather(slot_out, "slot", axis=0, tiled=True)

time: 139 us -> 139 us (level)
  blocking collectives: 85.1 us -> 89.9 us
  waiting for transfers between devices: 11.1 us -> 6.36 us
    all_gather x0 -> x1, blocking collectives: none -> 13.2 us  [body(): pieces = lax.all_gather(own, 'slot')]
    psum x1 -> x0, blocking collectives: 8.37 us -> none  [body(): lax.psum(jnp.sum(jnp.exp(logits - row_max[None, :]), axis=0), 'slot')]
    psum x1, waiting for transfers between devices: 11.1 us -> 6.34 us  [body(): numer, totals = lax.psum((numer, jnp.sum(dispatch_exp, axis=1)), 'tok')]
    reduce_sum x1 -> x2, other arithmetic: 4.57 us -> 4.59 us  [the longest x1 4.57 us: body(): own = jnp.sum(jnp.exp(logits - row_max[None, :]), axis=0)]
where the time goes in v1:
time: 139 us
  blocking collectives  89.9 us (65%)
  matrix products  14.3 us (10%)
  between operations  13.4 us (10%)
  waiting for transfers between devices  6.36 us (5%)
  other arithmetic  5.81 us (4%)
  local copies, waits for them, and re-layouts  5.44 us (4%)
  starting transfers between devices  3.28 us (2%)
    psum x1, blocking collectives, body(): slot_out = lax.psum(partial_out, 'tok').astype(jnp.bfloat16)  23.4 us
    pmax x1, blocking collectives, body(): col_max = lax.pmax(jnp.max(flight, axis=1), 'tok')  15.2 us
    all_gather x1, blocking collectives, body(): all_outputs = lax.all_gather(slot_out, 'slot', axis=0, tiled=True)  14.3 us
    all_gather x1, blocking collectives, body(): pieces = lax.all_gather(own, 'slot')  13.2 us
    pmax x1, blocking collectives, body(): row_max = lax.pmax(jnp.max(logits, axis=0), 'slot')  12 us
    psum x1, blocking collectives, body(): numer, totals = lax.psum((numer, jnp.sum(dispatch_exp, axis=1)), 'tok')  11.8 us
    dot_general x1, matrix products, body(): lax.dot_general(slot_params, tokens, (((1,), (1,)), ((), ())), preferred_...  6.37 us
    psum x1, waiting for transfers between devices, body(): numer, totals = lax.psum((numer, jnp.sum(dispatch_exp, axis=1)), 'tok')  6.34 us
  transfers between devices with their start and end apart: 2, of which 1 were waited for; matrix products, arithmetic and copies ran while one was open for 8% of the time, Pallas kernels for 0%

profile of v1, /device:TPU:0, one launch (start us, length us, event | category | flops | bytes accessed | tf_op | source)
XLA Modules:
  0.0 138.5 jit_solution(13865976925181170559)
XLA Ops:
  6.5 0.0 copy-start
  6.5 0.0 all-reduce.3.cloned.1.call-start
  6.5 1.6 %copy-done = bf16[1024,1024]{1,0:T(8,128)(2,1)S(1)} copy-done((bf16[1024,1024]{1,0:T(8,128)(2,1)S(1)}, bf16[1024,1024]{1,0:T(8,128)(2,1)}, u32[]{:S(2)}) %copy-start) | copy-done | bytes 2097176
  8.1 6.4 %fusion.27 = (f32[1024]{0:T(1024)S(1)}, f32[2048,1024]{1,0:T(8,128)S(1)}) fusion(bf16[2048,1024]{1,0:T(8,128)(2,1)} %param.5, bf16[1024,1024]{1,0:T(8,128)(2,1)S(1)} %copy-done), kind=kOutput, calls=%fused_computation.31 | convolution fusion | flops 4297063424 | bytes 14684160 | tf_op jit(solution)/shard_map/dot_general | solution.py:12
  14.5 0.0 copy-start.1
  14.5 3.2 %copy-done.1 = f32[2048,1024]{1,0:T(8,128)} copy-done((f32[2048,1024]{1,0:T(8,128)}, f32[2048,1024]{1,0:T(8,128)S(1)}, u32[]{:S(2)}) %copy-start.1) | copy-done | bytes 8388632
  17.7 0.1 slice_reduce_fusion
  17.8 15.2 %pmax.15 = f32[32]{0:T(128)S(1)} all-reduce(f32[32]{0:T(128)S(1)} %slice_reduce_fusion), channel_id=1, replica_groups=mesh['tok'=8,'slot'=4] {'tok'}, use_global_device_ids=true, to_apply=%region_5.0 | all-reduce | flops 32 | bytes 256 | tf_op jit(solution)/shard_map/pmax | solution.py:16
  33.0 2.1 %fusion.10 = f32[32,1024]{1,0:T(8,128)} fusion(bf16[1024,1024]{1,0:T(8,128)(2,1)S(1)} %copy-done, f32[2048,1024]{1,0:T(8,128)} %copy-done.1, f32[32]{0:T(128)S(1)} %pmax.15), kind=kOutput, calls=%fused_computation.18 | convolution fusion | flops 67174400 | bytes 2359424 | tf_op jit(solution)/shard_map/dot_general | solution.py:19
  35.1 0.0 all-reduce.3.cloned.1.call-update
  35.1 12.0 %pmax.14 = f32[1024]{0:T(1024)S(1)} all-reduce(f32[1024]{0:T(1024)S(1)} %get-tuple-element.7), channel_id=1, replica_groups=mesh['tok'=8,'slot'=4] {'slot'}, use_global_device_ids=true, to_apply=%region_1.0 | all-reduce | flops 1024 | bytes 8192 | tf_op jit(solution)/shard_map/pmax | solution.py:29
  47.1 4.6 %exponential_reduce_fusion = f32[1024]{0:T(1024)S(1)} fusion(f32[2048,1024]{1,0:T(8,128)} %copy-done.1, f32[1024]{0:T(1024)S(1)} %pmax.14), kind=kLoop, calls=%fused_computation | loop fusion | flops 4193280 | bytes 8396800 | tf_op jit(solution)/shard_map/reduce_sum | solution.py:30
  51.6 13.2 %all-gather = f32[4096]{0:T(1024)S(1)} all-gather(f32[1024]{0:T(1024)S(1)} %exponential_reduce_fusion), channel_id=2, replica_groups=mesh['tok'=8,'slot'=4] {'slot'}, dimensions={0}, use_global_device_ids=true | all-gather | bytes 20480 | tf_op jit(solution)/shard_map/all_gather | solution.py:31
  64.9 1.1 fusion
  66.0 0.6 copy.10
  66.6 3.3 %all-to-all-start = ((bf16[32,4,256]{2,0,1:T(8,128)(2,1)}), bf16[32,4,256]{2,0,1:T(8,128)(2,1)S(1)}, u32[]{:S(2)}, u32[]{:S(2)}) async-start(bf16[32,4,256]{2,0,1:T(8,128)(2,1)} %bitcast.22), calls=%async_computation | async-start | bytes 131072 | tf_op jit(solution)/shard_map/all_to_all | solution.py:34
  69.9 11.8 %psum.22 = f32[32]{0:T(128)S(1)} all-reduce(f32[32]{0:T(128)S(1)} %get-tuple-element.5), channel_id=1, replica_groups=mesh['tok'=8,'slot'=4] {'tok'}, use_global_device_ids=true, to_apply=%region_8.0 | all-reduce | flops 32 | bytes 256 | tf_op jit(solution)/shard_map/psum | solution.py:20
  81.7 6.3 %all-reduce.3.cloned.1.call-done = f32[32,1024]{1,0:T(8,128)} async-done(((f32[32,1024]{1,0:T(8,128)}), f32[32,1024]{1,0:T(8,128)}) %all-reduce.3.cloned.1.call-update) | async-done | bytes 131088 | tf_op jit(solution)/shard_map/psum | solution.py:20
  88.1 4.7 %convolution_bitcast_fusion = f32[32,1024]{1,0:T(8,128)S(1)} fusion(bf16[4,512,1024]{2,1,0:T(8,128)(2,1)} %param.7, bf16[4,1024,512]{2,1,0:T(8,128)(2,1)} %param.6, f32[32,1024]{1,0:T(8,128)} %all-reduce.3.cloned.1.call-done, f32[32]{0:T(128)S(1)} %psum.22), kind=kOutput, calls=%fused_computation.2 | convolution fusion | flops 67321856 | bytes 8650880 | tf_op jit(solution)/shard_map/eph,ehd->epd/dot_general | solution.py:26
  92.8 23.4 %all-reduce.4 = bf16[32,1024]{1,0:T(8,128)(2,1)S(1)} all-reduce(f32[32,1024]{1,0:T(8,128)S(1)} %convolution_bitcast_fusion), channel_id=1, replica_groups=mesh['tok'=8,'slot'=4] {'tok'}, use_global_device_ids=true, to_apply=%region_9.0 | all-reduce | flops 32768 | bytes 196608 | tf_op jit(solution)/shard_map/psum | solution.py:28
  116.3 14.3 %all_gather.11 = bf16[128,1024]{1,0:T(8,128)(2,1)S(1)} all-gather(bf16[32,1024]{1,0:T(8,128)(2,1)S(1)} %all-reduce.4), channel_id=1, replica_groups=mesh['tok'=8,'slot'=4] {'slot'}, dimensions={0}, use_global_device_ids=true | all-gather | bytes 327680 | tf_op jit(solution)/shard_map/all_gather | solution.py:35
  130.6 0.0 all-to-all-done
  130.6 1.1 convolution_convert_fusion
  (2 shorter events, 0.0 us)
Async XLA Ops:
  6.5 1.6 %copy-start = (bf16[1024,1024]{1,0:T(8,128)(2,1)S(1)}, bf16[1024,1024]{1,0:T(8,128)(2,1)}, u32[]{:S(2)}) copy-start(bf16[1024,1024]{1,0:T(8,128)(2,1)} %param.4) | copy-start | bytes 6291460
  6.5 81.5 %all-reduce.3.cloned.1.call-start = ((), (), s32[]{:S(2)}) async-start(), calls=%async_computation.1 | async-start | bytes 262144 | tf_op jit(solution)/shard_map/psum | solution.py:20
  14.5 3.2 %copy-start.1 = (f32[2048,1024]{1,0:T(8,128)}, f32[2048,1024]{1,0:T(8,128)S(1)}, u32[]{:S(2)}) copy-start(f32[2048,1024]{1,0:T(8,128)S(1)} %get-tuple-element.8) | copy-start | bytes 25165828
  66.6 63.9 %all-to-all-start = ((bf16[32,4,256]{2,0,1:T(8,128)(2,1)}), bf16[32,4,256]{2,0,1:T(8,128)(2,1)S(1)}, u32[]{:S(2)}, u32[]{:S(2)}) async-start(bf16[32,4,256]{2,0,1:T(8,128)(2,1)} %bitcast.22), calls=%async_computation | async-start | bytes 131072 | tf_op jit(solution)/shard_map/all_to_all | solution.py:34
Sparse Core Ops, SparseCore 0:
  35.2 52.7 all-reduce.2
